TPU v7x, 32 devices: a whole 2x2x4 slice. The times are simulated.
32 devices in a mesh: trans: 16 (over z, y, x), los: 2 (over core).
Axes of the slice: x: 2, y: 2, z: 4, core: 2. Of those that a mesh axis runs over, the one named last changes fastest.
Arguments:
- density: bfloat16 [2, 2048, 2048], P('los', 'trans'), may hold values from -6 to 6
- row_pos: float32 [2, 2048], replicated, may hold values from 0 to 2048
- col_pos: float32 [2, 2048], replicated, may hold values from 0 to 2048
- plane_of_slot: int32 [2], replicated, may hold values from 0 to 1, each once
- plane_bin: int32 [2], replicated, may hold values from 0 to 3, as said below
- efficiency: float32 [4, 2], replicated, may hold values from 0.3 to 3
Outputs:
- shear: float32 [2, 4, 2048, 2048], P(None, None, ('trans', 'los'))
Inputs may be any that keep to these rules, and one draw needn't show every extreme that they name: `plane_bin`: some plane has bin 0 and some plane has bin 4 - 1.
All inputs are finite; a program needn't handle non-finite values.
Results may differ from a plain program's by a relative error of at most 0.006.
Values may be sent and summed in bfloat16 or wider, within the bound.
A program may use at most 64 MiB of HBM per device.

v0:
```python
import math
import jax
import jax.numpy as jnp
from jax import lax
from jax.sharding import PartitionSpec as P


def hat_block(positions, mesh_cells):
    cells = jnp.arange(mesh_cells, dtype=jnp.int32).astype(jnp.float32)
    offset = positions[:, None] - cells[None, :] + 0.5 * mesh_cells
    folded = jnp.mod(offset, 1.0 * mesh_cells) - 0.5 * mesh_cells
    return jnp.maximum(1.0 - jnp.abs(folded), 0.0).astype(jnp.bfloat16)


def trig_pair(rows_n, cols_n, modulus, sign_value):
    product_index = (
        jnp.arange(rows_n, dtype=jnp.int32)[:, None]
        * jnp.arange(cols_n, dtype=jnp.int32)[None, :]
        % modulus
    )
    angle = product_index.astype(jnp.float32) * (2.0 * math.pi / modulus)
    return (jnp.cos(angle), sign_value * jnp.sin(angle))


def fourier(real_part, imag_part, inverse):
    length = real_part.shape[-1]
    factor_one = 16
    second = length // factor_one
    sign_value = 1.0 if inverse else -1.0
    lead_shape = real_part.shape[:-1]
    highest = lax.Precision.HIGHEST
    cos_one, sin_one = trig_pair(factor_one, factor_one, factor_one, sign_value)
    real_grid = real_part.reshape(lead_shape + (factor_one, second))
    imag_grid = imag_part.reshape(lead_shape + (factor_one, second))

    def first_pass(table, values):
        return jnp.einsum("kn,...nm->...km", table, values, precision=highest)

    section_real = first_pass(cos_one, real_grid) - first_pass(sin_one, imag_grid)
    section_imag = first_pass(cos_one, imag_grid) + first_pass(sin_one, real_grid)
    cos_twid, sin_twid = trig_pair(factor_one, second, length, sign_value)
    turned_real = section_real * cos_twid - section_imag * sin_twid
    turned_imag = section_real * sin_twid + section_imag * cos_twid
    cos_two, sin_two = trig_pair(second, second, second, sign_value)

    def second_pass(values, table):
        return jnp.einsum("...km,mj->...kj", values, table, precision=highest)

    out_real = second_pass(turned_real, cos_two) - second_pass(turned_imag, sin_two)
    out_imag = second_pass(turned_real, sin_two) + second_pass(turned_imag, cos_two)
    out_real = jnp.swapaxes(out_real, -1, -2).reshape(lead_shape + (length,))
    out_imag = jnp.swapaxes(out_imag, -1, -2).reshape(lead_shape + (length,))
    scale = 1.0 / length if inverse else 1.0
    return (out_real * scale, out_imag * scale)


def wave_numbers(index_all, length):
    return jnp.where(index_all < length // 2, index_all, index_all - length).astype(jnp.float32)


def body(density, row_pos, col_pos, plane_of_slot, plane_bin, efficiency):
    count_trans = lax.axis_size("trans")
    count_los = lax.axis_size("los")
    per_device = density.shape[0]
    mesh_cells = density.shape[2]
    grid_cells = row_pos.shape[1]
    planes_total = row_pos.shape[0]
    bins_total = efficiency.shape[0]
    width_cols = grid_cells // (count_trans * count_los)
    block_rows = min(512, grid_cells)
    slots = jnp.arange(planes_total, dtype=jnp.int32)
    bin_index = jnp.arange(bins_total, dtype=jnp.int32)
    by_columns = lax.all_to_all(density, "trans", split_axis=2, concat_axis=1, tiled=True)
    local_slot = 0
    slot_now = lax.axis_index("los") * per_device + local_slot
    plane_id = jnp.sum(jnp.where(slots == slot_now, plane_of_slot, 0))
    chosen = slots == plane_id
    plane_eff = jnp.sum(jnp.where(chosen[None, :], efficiency, 0.0), axis=1)
    first_bin = jnp.sum(jnp.where(chosen, plane_bin, 0))
    weight_list = [plane_eff * (bin_index >= first_bin).astype(jnp.float32)]
    rows_here = jnp.sum(jnp.where(chosen[:, None], row_pos, 0.0), axis=0)
    cols_here = jnp.sum(jnp.where(chosen[:, None], col_pos, 0.0), axis=0)
    pieces = []
    for begin in range(0, grid_cells, block_rows):
        row_block = hat_block(rows_here[begin : begin + block_rows], mesh_cells)
        pieces.append(
            lax.dot_general(
                by_columns[local_slot],
                row_block,
                (((0,), (1,)), ((), ())),
                preferred_element_type=jnp.float32,
            )
        )
    resampled = [jnp.concatenate(pieces, axis=1).astype(jnp.bfloat16)]
    col_tables = [hat_block(cols_here, mesh_cells)]
    half_columns = jnp.stack(resampled)
    exchanged = lax.all_to_all(half_columns, "trans", split_axis=2, concat_axis=1, tiled=True)
    local_slot = 0
    rows_map = lax.dot_general(
        exchanged[local_slot],
        col_tables[local_slot],
        (((0,), (1,)), ((), ())),
        preferred_element_type=jnp.float32,
    )
    plane_term = weight_list[local_slot][None, :, None] * rows_map[:, None, :]
    term_real, term_imag = fourier(plane_term, jnp.zeros_like(plane_term), False)
    summed_real, summed_imag = (
        lax.psum_scatter(term_real, "los", scatter_dimension=2, tiled=True),
        lax.psum_scatter(term_imag, "los", scatter_dimension=2, tiled=True),
    )
    arrived = lax.all_to_all(
        jnp.stack([summed_real, summed_imag]), "trans", split_axis=3, concat_axis=1, tiled=True
    )
    columns_local = arrived.transpose(0, 2, 3, 1)
    col_index = (
        lax.axis_index("los") * (grid_cells // count_los)
        + lax.axis_index("trans") * width_cols
        + jnp.arange(width_cols, dtype=jnp.int32)
    )
    freq_real, freq_imag = fourier(columns_local[0], columns_local[1], False)
    wave_rows = wave_numbers(jnp.arange(grid_cells, dtype=jnp.int32), grid_cells)[None, :]
    wave_cols = wave_numbers(col_index, grid_cells)[:, None]
    square_sum = jnp.maximum(wave_rows * wave_rows + wave_cols * wave_cols, 1.0)
    first_factor = (wave_rows * wave_rows - wave_cols * wave_cols) / square_sum
    second_factor = 2.0 * wave_rows * wave_cols / square_sum
    kernel_real = first_factor * freq_real - second_factor * freq_imag
    kernel_imag = first_factor * freq_imag + second_factor * freq_real
    back_real, back_imag = fourier(kernel_real, kernel_imag, True)
    returned = jnp.stack([back_real, back_imag]).transpose(0, 3, 1, 2)
    rows_local = lax.all_to_all(
        lax.all_to_all(returned, "trans", split_axis=1, concat_axis=3, tiled=True),
        "los",
        split_axis=1,
        concat_axis=3,
        tiled=True,
    )
    final_real, final_imag = fourier(rows_local[0], rows_local[1], True)
    return jnp.stack([final_real, final_imag]).transpose(0, 2, 1, 3)


def solution(mesh):
    placed = (P("los", "trans", None), P(), P(), P(), P(), P())
    return jax.shard_map(
        body,
        mesh=mesh,
        in_specs=placed,
        out_specs=P(None, None, ("trans", "los"), None),
        check_vma=False,
    )
```

profile of v0, /device:TPU:0, one launch (start us, length us, event | category | flops | bytes accessed | tf_op | source)
XLA Modules:
  0.0 628.0 jit_solution(389081637381458077)
XLA Ops:
  9.4 11.4 %reduce = bf16[2048,128]{1,0:T(8,128)(2,1)S(1)} reduce(bf16[2048,1,128]{2,1,0:T(2,128)(2,1)S(1)} %bitcast.333, bf16[]{:T(256)} %broadcast.788), dimensions={1}, to_apply=%bitcast.274.reduce_sub_computation | reduce | bytes 1048578
  21.8 8.9 %all-to-all-start = ((bf16[16,2,8192]{2,1,0:T(2,128)(2,1)}), bf16[16,2,8192]{2,1,0:T(2,128)(2,1)S(1)}, u32[]{:S(2)}, u32[]{:S(2)}) async-start(bf16[16,2,8192]{2,1,0:T(2,128)(2,1)} %reshape.416), calls=%async_computation | async-start | bytes 1048576 | tf_op jit(solution)/shard_map/all_to_all | solution.py:73
  32.2 13.6 %all-to-all-done = bf16[16,2,8192]{2,1,0:T(2,128)(2,1)S(1)} async-done(((bf16[16,2,8192]{2,1,0:T(2,128)(2,1)}), bf16[16,2,8192]{2,1,0:T(2,128)(2,1)S(1)}, u32[]{:S(2)}, u32[]{:S(2)}) %all-to-all-start) | async-done | bytes 524320 | tf_op jit(solution)/shard_map/all_to_all | solution.py:73
  61.7 8.1 %copy.182 = bf16[1,128,2048]{1,0,2:T(2,128)(2,1)S(1)} copy(bf16[1,128,2048]{1,2,0:T(8,128)(2,1)S(1)} %pad_maximum_fusion.1) | data formatting | bytes 1048576 | tf_op jit(solution)/shard_map/concatenate | solution.py:94
  69.9 11.6 %reduce.1 = bf16[2048,128]{1,0:T(8,128)(2,1)S(1)} reduce(bf16[2048,1,128]{2,1,0:T(2,128)(2,1)S(1)} %bitcast.334, bf16[]{:T(256)} %broadcast.788), dimensions={1}, to_apply=%bitcast.300.reduce_sub_computation | reduce | bytes 1048578
  88.5 12.4 %all-to-all-done.1 = bf16[16,2,8192]{2,1,0:T(2,128)(2,1)S(1)} async-done(((bf16[16,2,8192]{2,1,0:T(2,128)(2,1)}), bf16[16,2,8192]{2,1,0:T(2,128)(2,1)S(1)}, u32[]{:S(2)}, u32[]{:S(2)}) %all-to-all-start.1) | async-done | bytes 524320 | tf_op jit(solution)/shard_map/all_to_all | solution.py:97
  102.0 12.7 %fusion.8 = f32[128,16,128]{2,0,1:T(8,128)S(1)} fusion(bf16[2048,128,1]{0,1,2:T(8,128)(2,1)S(1)} %reshape.400, f32[2048]{0:T(1024)S(1)} %iota_convert_fusion, f32[16,128]{1,0:T(8,128)S(1)} %bitcast.343), kind=kOutput, calls=%fused_computation.12 | convolution fusion | flops 1128267776 | bytes 1589248 | tf_op jit(solution)/shard_map/dot_general | solution.py:99
  128.5 6.5 %fusion.52 = f32[128,4,16,128]{0,3,2,1:T(8,128)S(1)} fusion(f32[128,4,16,128]{3,2,1,0:T(8,128)S(1)} %get-tuple-element.10), kind=kOutput, calls=%fused_computation.75 | convolution fusion | flops 1610858496 | bytes 8388608 | tf_op jit(solution)/shard_map/...km,mj->...kj/dot_general | solution.py:47
  135.1 6.7 %subtract_bitcast_fusion = f32[128,4,128,16]{0,2,3,1:T(8,128)S(1)} fusion(f32[128,4,16,128]{0,3,2,1:T(8,128)S(1)} %fusion.52, f32[128,4,16,128]{3,2,1,0:T(8,128)S(1)} %get-tuple-element.9), kind=kOutput, calls=%fused_computation.56 | convolution fusion | flops 1611890688 | bytes 12582912 | tf_op jit(solution)/shard_map/...km,mj->...kj/dot_general | solution.py:47
  146.2 9.4 %fusion.50 = f32[128,4,16,128]{0,3,2,1:T(8,128)S(1)} fusion(f32[128,4,16,128]{3,2,1,0:T(8,128)} %copy-done.5), kind=kOutput, calls=%fused_computation.73 | convolution fusion | flops 1610842112 | bytes 8388608 | tf_op jit(solution)/shard_map/...km,mj->...kj/dot_general | solution.py:47
  155.7 6.5 %add_bitcast_fusion = f32[128,4,128,16]{0,2,3,1:T(8,128)S(1)} fusion(f32[128,4,16,128]{0,3,2,1:T(8,128)S(1)} %fusion.50, f32[128,4,16,128]{3,2,1,0:T(8,128)S(1)} %copy-done.4), kind=kOutput, calls=%fused_computation.55 | convolution fusion | flops 1611907072 | bytes 12582912 | tf_op jit(solution)/shard_map/...km,mj->...kj/dot_general | solution.py:47
  166.7 10.4 %reduce-scatter.5.cloned.1.call-done = f32[128,4,1024]{0,2,1:T(8,128)} async-done(((f32[128,4,2048]{0,2,1:T(8,128)}), f32[128,4,1024]{0,2,1:T(8,128)}) %reduce-scatter.5.cloned.1.call-update) | async-done | bytes 2097168 | tf_op jit(solution)/shard_map/reduce_scatter | solution.py:109
  179.7 4.9 copy.123
  184.6 7.0 %all-to-all-start.2 = ((f32[2,128,4,1024]{1,2,0,3:T(4,128)}), f32[2,128,4,1024]{1,2,0,3:T(4,128)}, u32[]{:S(2)}, u32[]{:S(2)}) async-start(f32[2,128,4,1024]{1,2,0,3:T(4,128)} %copy.123), calls=%async_computation.4 | async-start | bytes 8388608 | tf_op jit(solution)/shard_map/all_to_all | solution.py:111
  193.2 78.7 %all-to-all-done.2 = f32[2,128,4,1024]{1,2,0,3:T(4,128)} async-done(((f32[2,128,4,1024]{1,2,0,3:T(4,128)}), f32[2,128,4,1024]{1,2,0,3:T(4,128)}, u32[]{:S(2)}, u32[]{:S(2)}) %all-to-all-start.2) | async-done | bytes 4194336 | tf_op jit(solution)/shard_map/all_to_all | solution.py:111
  298.5 5.6 add_bitcast_fusion.1
  304.1 4.5 copy.127
  308.6 8.7 %fusion.34 = (f32[4,64,16,128]{1,3,2,0:T(8,128)}, f32[4,64,16,128]{1,3,2,0:T(8,128)}) fusion(f32[64,16,128]{0,2,1:T(8,128)S(1)} %copy-done.15, f32[64,16,128]{0,2,1:T(8,128)S(1)} %get-tuple-element.15, f32[4,64,16,128]{1,3,2,0:T(8,128)} %bitcast.325, f32[4,64,16,128]{1,3,2,0:T(8,128)} %bitcast.323), kind=kLoop, calls=%fused_computation.45 | loop fusion | flops 3145728 | bytes 9437184 | tf_op jit(solution)/shard_map/sub | solution.py:126
  349.9 5.6 multiply_bitcast_fusion.2
  364.1 15.3 %copy.181 = f32[2,2048,4,64]{3,2,0,1:T(4,128)} copy(f32[2,2048,4,64]{3,1,2,0:T(8,128)S(1)} %maximum_bitcast_fusion) | data formatting | bytes 8388608 | tf_op jit(solution)/shard_map/transpose | solution.py:129
  379.4 14.6 %reshape.420 = f32[16,1,65536]{2,1,0:T(1,128)} reshape(f32[2048,2,4,64]{3,2,1,0:T(4,128)} %bitcast.312) | data formatting | bytes 8388608
  393.9 113.6 %all_to_all.81 = f32[16,1,65536]{2,1,0:T(1,128)} all-to-all(f32[16,1,65536]{2,1,0:T(1,128)} %reshape.420), channel_id=1, replica_groups=mesh['trans'=16,'los'=2] {'trans'}, dimensions={0} | all-to-all | bytes 8388608 | tf_op jit(solution)/shard_map/all_to_all | solution.py:131
  508.2 13.8 %reduce.2 = f32[16,65536]{1,0:T(8,128)} reduce(f32[16,1,65536]{2,1,0:T(1,128)} %all_to_all.81, f32[]{:T(128)} %broadcast.790), dimensions={1}, to_apply=%all_to_all.69.reduce_sub_computation | reduce | bytes 8388612 | tf_op jit(solution)/shard_map/all_to_all | solution.py:131
  522.0 9.3 %reshape.421 = f32[2048,2,4,64]{3,2,1,0:T(4,128)} reshape(f32[16,65536]{1,0:T(8,128)} %reduce.2) | data formatting | bytes 8388608
  531.2 8.5 %copy.159 = f32[2,16,128,4,64]{2,4,1,3,0:T(8,128)} copy(f32[2,16,128,4,64]{4,3,0,2,1:T(4,128)} %bitcast.311) | data formatting | bytes 8388608 | tf_op jit(solution)/shard_map/all_to_all | solution.py:131
  539.7 5.5 copy.137
  545.3 8.6 %all_to_all.82 = f32[2,128,4,1024]{3,2,0,1:T(4,128)S(1)} all-to-all(f32[2,128,4,1024]{3,2,0,1:T(4,128)} %copy.137), channel_id=1, replica_groups=mesh['trans'=16,'los'=2] {'los'}, dimensions={1} | all-to-all | bytes 8388608 | tf_op jit(solution)/shard_map/all_to_all | solution.py:130
  591.7 4.8 copy.141
  596.5 5.6 multiply_bitcast_fusion
  602.1 4.8 copy.142
  606.9 7.2 %maximum_bitcast_fusion.1 = f32[2,4,64,2048]{2,3,1,0:T(8,128)} fusion(f32[1,64,4,2048]{1,3,2,0:T(8,128)} %bitcast.328, f32[1,64,4,2048]{1,3,2,0:T(8,128)} %bitcast.324), kind=kLoop, calls=%fused_computation.11 | loop fusion | flops 1048576 | bytes 8388608 | tf_op jit(solution)/shard_map/transpose | solution.py:138
  614.1 6.8 %copy.143 = f32[2,4,64,2048]{3,2,1,0:T(8,128)} copy(f32[2,4,64,2048]{2,3,1,0:T(8,128)} %maximum_bitcast_fusion.1) | data formatting | bytes 8388608 | tf_op jit(solution)/shard_map/transpose | solution.py:138
  (125 shorter events, 161.8 us)
Async XLA Ops:
  8.9 21.8 %copy-start.19 = (s32[2]{0:T(128)S(1)}, s32[2]{0:T(128)}, u32[]{:S(2)}) copy-start(s32[2]{0:T(128)} %param.9) | copy-start | bytes 28
  8.9 23.1 %copy-start.16 = (f32[2,2048]{1,0:T(2,128)S(1)}, f32[2,2048]{1,0:T(2,128)}, u32[]{:S(2)}) copy-start(f32[2,2048]{1,0:T(2,128)} %param.8) | copy-start | bytes 49156
  8.9 23.1 %copy-start.17 = (f32[2,2048]{1,0:T(2,128)S(1)}, f32[2,2048]{1,0:T(2,128)}, u32[]{:S(2)}) copy-start(f32[2,2048]{1,0:T(2,128)} %param.7) | copy-start | bytes 49156
  21.8 23.9 %all-to-all-start = ((bf16[16,2,8192]{2,1,0:T(2,128)(2,1)}), bf16[16,2,8192]{2,1,0:T(2,128)(2,1)S(1)}, u32[]{:S(2)}, u32[]{:S(2)}) async-start(bf16[16,2,8192]{2,1,0:T(2,128)(2,1)} %reshape.416), calls=%async_computation | async-start | bytes 1048576 | tf_op jit(solution)/shard_map/all_to_all | solution.py:73
  69.9 16.6 %copy-start.20 = (s32[2]{0:T(128)S(1)}, s32[2]{0:T(128)}, u32[]{:S(2)}) copy-start(s32[2]{0:T(128)} %param.10) | copy-start | bytes 28
  69.9 17.9 %copy-start.18 = (f32[4,2]{0,1:T(2,128)S(1)}, f32[4,2]{0,1:T(2,128)}, u32[]{:S(2)}) copy-start(f32[4,2]{0,1:T(2,128)} %param.11) | copy-start | bytes 100
  82.4 18.4 %all-to-all-start.1 = ((bf16[16,2,8192]{2,1,0:T(2,128)(2,1)}), bf16[16,2,8192]{2,1,0:T(2,128)(2,1)S(1)}, u32[]{:S(2)}, u32[]{:S(2)}) async-start(bf16[16,2,8192]{2,1,0:T(2,128)(2,1)} %reshape.418), calls=%async_computation.1 | async-start | bytes 1048576 | tf_op jit(solution)/shard_map/all_to_all | solution.py:97
  86.4 80.3 %reduce-scatter.3.cloned.1.call-start = ((), (), s32[]{:S(2)}) async-start(), calls=%async_computation.7 | async-start | bytes 6291456 | tf_op jit(solution)/shard_map/reduce_scatter | solution.py:108
  128.5 6.5 %copy-start.5 = (f32[128,4,16,128]{3,2,1,0:T(8,128)}, f32[128,4,16,128]{3,2,1,0:T(8,128)S(1)}, u32[]{:S(2)}) copy-start(f32[128,4,16,128]{3,2,1,0:T(8,128)S(1)} %get-tuple-element.10) | copy-start | bytes 12582916
  128.5 6.5 %copy-start.3 = (f32[128,4,16,128]{3,2,1,0:T(8,128)}, f32[128,4,16,128]{3,2,1,0:T(8,128)S(1)}, u32[]{:S(2)}) copy-start(f32[128,4,16,128]{3,2,1,0:T(8,128)S(1)} %get-tuple-element.9) | copy-start | bytes 12582916
  146.2 31.0 %reduce-scatter.5.cloned.1.call-start = ((), (), s32[]{:S(2)}) async-start(), calls=%async_computation.8 | async-start | bytes 6291456 | tf_op jit(solution)/shard_map/reduce_scatter | solution.py:109
  146.2 9.5 %copy-start.4 = (f32[128,4,16,128]{3,2,1,0:T(8,128)S(1)}, f32[128,4,16,128]{3,2,1,0:T(8,128)}, u32[]{:S(2)}) copy-start(f32[128,4,16,128]{3,2,1,0:T(8,128)} %copy-done.3) | copy-start | bytes 12582916
  184.6 87.3 %all-to-all-start.2 = ((f32[2,128,4,1024]{1,2,0,3:T(4,128)}), f32[2,128,4,1024]{1,2,0,3:T(4,128)}, u32[]{:S(2)}, u32[]{:S(2)}) async-start(f32[2,128,4,1024]{1,2,0,3:T(4,128)} %copy.123), calls=%async_computation.4 | async-start | bytes 8388608 | tf_op jit(solution)/shard_map/all_to_all | solution.py:111
  284.6 6.0 copy-start.1
  304.1 4.5 copy-start.15
  320.4 3.3 copy-start.6
  327.0 1.3 copy-start.8
  328.3 2.0 copy-start.13
  330.2 3.7 copy-start.7
  336.0 5.6 copy-start.2
  564.0 3.3 copy-start.9
  564.0 3.3 copy-start.14
  573.4 1.3 copy-start.11
  574.7 2.0 copy-start.12
  576.7 3.7 copy-start.10
  582.4 5.6 copy-start
Sparse Core Ops, SparseCore 0:
  146.3 10.2 reduce-scatter.2
  166.8 10.2 reduce-scatter.4
where the time goes:
time: 634 us; the launch traced here: 628 us
  local copies, waits for them, and re-layouts  147 us (23%)
  matrix products  145 us (23%)
  blocking collectives  122 us (19%)
  waiting for transfers between devices  115 us (18%)
  other arithmetic  64.5 us (10%)
  starting transfers between devices  19.9 us (3%)
  between operations  14.4 us (2%)
    all_to_all x1, blocking collectives, body(): lax.all_to_all(returned, 'trans', split_axis=1, concat_axis=3, tiled=True)  114 us
    all_to_all x1, waiting for transfers between devices, body(): lax.all_to_all(jnp.stack([summed_real, summed_imag]), 'trans', split_axis...  78.7 us
    dot_general x16, matrix products, second_pass(): return jnp.einsum('...km,mj->...kj', values, table, precision=highest)  74.2 us
    dot_general x16, matrix products, first_pass(): return jnp.einsum('kn,...nm->...km', table, values, precision=highest)  42.8 us
    unnamed x54, local copies, waits for them, and re-layouts  33.2 us
    unnamed x2, other arithmetic  23.1 us
    mul x4, local copies, waits for them, and re-layouts, fourier(): return (out_real * scale, out_imag * scale)  18.3 us
    transpose x1, local copies, waits for them, and re-layouts, body(): returned = jnp.stack([back_real, back_imag]).transpose(0, 3, 1, 2)  15.3 us
  transfers between devices with their start and end apart: 5, of which 4 were waited for; matrix products, arithmetic and copies ran while one was open for 4% of the time, Pallas kernels for 0%

commit v1 on v0

--- a/solution.py
+++ b/solution.py
@@ -127,12 +127,17 @@
     kernel_imag = first_factor * freq_imag + second_factor * freq_real
     back_real, back_imag = fourier(kernel_real, kernel_imag, True)
     returned = jnp.stack([back_real, back_imag]).transpose(0, 3, 1, 2)
-    rows_local = lax.all_to_all(
-        lax.all_to_all(returned, "trans", split_axis=1, concat_axis=3, tiled=True),
-        "los",
-        split_axis=1,
-        concat_axis=3,
-        tiled=True,
+    signs_proceed = lambda shard_in: jnp.concatenate(
+        lax.all_to_all(
+            jnp.stack(jnp.split(shard_in, lax.psum(1, axis_name="los"), axis=1), axis=0),
+            split_axis=0,
+            concat_axis=0,
+            axis_name="los",
+        ),
+        axis=3,
+    )
+    rows_local = signs_proceed(
+        lax.all_to_all(returned, "trans", split_axis=1, concat_axis=3, tiled=True)
     )
     final_real, final_imag = fourier(rows_local[0], rows_local[1], True)
     return jnp.stack([final_real, final_imag]).transpose(0, 2, 1, 3)

time: 634 us -> 642 us (1.013)
    another operation x0 -> x2, local copies, waits for them, and re-layouts: none -> 11.6 us  [body(): jnp.stack(jnp.split(shard_in, lax.psum(1, axis_name='los'), axis=1), axis=0)]
    all_to_all x3 -> x2, local copies, waits for them, and re-layouts: 14.6 us -> 9.07 us  [body(): lax.all_to_all(returned, 'trans', split_axis=1, concat_axis=3, tiled=True)]
where the time goes in v1:
time: 642 us; the launch traced here: 636 us
  local copies, waits for them, and re-layouts  151 us (24%)
  matrix products  144 us (22%)
  blocking collectives  122 us (19%)
  waiting for transfers between devices  115 us (18%)
  other arithmetic  68.8 us (11%)
  starting transfers between devices  19.6 us (3%)
  between operations  14.6 us (2%)
    all_to_all x1, blocking collectives, body(): lax.all_to_all(returned, 'trans', split_axis=1, concat_axis=3, tiled=True)  114 us
    all_to_all x1, waiting for transfers between devices, body(): lax.all_to_all(jnp.stack([summed_real, summed_imag]), 'trans', split_axis...  78.7 us
    dot_general x16, matrix products, second_pass(): return jnp.einsum('...km,mj->...kj', values, table, precision=highest)  74.1 us
    dot_general x16, matrix products, first_pass(): return jnp.einsum('kn,...nm->...km', table, values, precision=highest)  42.8 us
    unnamed x54, local copies, waits for them, and re-layouts  33.2 us
    unnamed x2, other arithmetic  23.5 us
    mul x4, local copies, waits for them, and re-layouts, fourier(): return (out_real * scale, out_imag * scale)  18.4 us
    transpose x1, local copies, waits for them, and re-layouts, body(): returned = jnp.stack([back_real, back_imag]).transpose(0, 3, 1, 2)  15.3 us
  transfers between devices with their start and end apart: 5, of which 4 were waited for; matrix products, arithmetic and copies ran while one was open for 4% of the time, Pallas kernels for 0%

profile of v1, /device:TPU:0, one launch (start us, length us, event | category | flops | bytes accessed | tf_op | source)
XLA Modules:
  0.0 635.9 jit_solution(4881082690271037705)
XLA Ops:
  9.5 11.5 %reduce = bf16[2048,128]{1,0:T(8,128)(2,1)S(1)} reduce(bf16[2048,1,128]{2,1,0:T(2,128)(2,1)S(1)} %bitcast.335, bf16[]{:T(256)} %broadcast.788), dimensions={1}, to_apply=%bitcast.276.reduce_sub_computation | reduce | bytes 1048578
  21.9 8.6 %all-to-all-start = ((bf16[16,2,8192]{2,1,0:T(2,128)(2,1)}), bf16[16,2,8192]{2,1,0:T(2,128)(2,1)S(1)}, u32[]{:S(2)}, u32[]{:S(2)}) async-start(bf16[16,2,8192]{2,1,0:T(2,128)(2,1)} %reshape.421), calls=%async_computation | async-start | bytes 1048576 | tf_op jit(solution)/shard_map/all_to_all | solution.py:73
  31.9 13.7 %all-to-all-done = bf16[16,2,8192]{2,1,0:T(2,128)(2,1)S(1)} async-done(((bf16[16,2,8192]{2,1,0:T(2,128)(2,1)}), bf16[16,2,8192]{2,1,0:T(2,128)(2,1)S(1)}, u32[]{:S(2)}, u32[]{:S(2)}) %all-to-all-start) | async-done | bytes 524320 | tf_op jit(solution)/shard_map/all_to_all | solution.py:73
  61.5 8.1 %copy.183 = bf16[1,128,2048]{1,0,2:T(2,128)(2,1)S(1)} copy(bf16[1,128,2048]{1,2,0:T(8,128)(2,1)S(1)} %pad_maximum_fusion.2) | data formatting | bytes 1048576 | tf_op jit(solution)/shard_map/concatenate | solution.py:94
  69.7 12.0 %reduce.1 = bf16[2048,128]{1,0:T(8,128)(2,1)S(1)} reduce(bf16[2048,1,128]{2,1,0:T(2,128)(2,1)S(1)} %bitcast.336, bf16[]{:T(256)} %broadcast.788), dimensions={1}, to_apply=%bitcast.302.reduce_sub_computation | reduce | bytes 1048578
  88.6 12.3 %all-to-all-done.1 = bf16[16,2,8192]{2,1,0:T(2,128)(2,1)S(1)} async-done(((bf16[16,2,8192]{2,1,0:T(2,128)(2,1)}), bf16[16,2,8192]{2,1,0:T(2,128)(2,1)S(1)}, u32[]{:S(2)}, u32[]{:S(2)}) %all-to-all-start.1) | async-done | bytes 524320 | tf_op jit(solution)/shard_map/all_to_all | solution.py:97
  102.2 12.5 %fusion.8 = f32[128,16,128]{2,0,1:T(8,128)S(1)} fusion(bf16[2048,128,1]{0,1,2:T(8,128)(2,1)S(1)} %reshape.405, f32[2048]{0:T(1024)S(1)} %iota_convert_fusion, f32[16,128]{1,0:T(8,128)S(1)} %bitcast.345), kind=kOutput, calls=%fused_computation.13 | convolution fusion | flops 1128267776 | bytes 1589248 | tf_op jit(solution)/shard_map/dot_general | solution.py:99
  128.5 6.5 %fusion.52 = f32[128,4,16,128]{0,3,2,1:T(8,128)S(1)} fusion(f32[128,4,16,128]{3,2,1,0:T(8,128)S(1)} %get-tuple-element.10), kind=kOutput, calls=%fused_computation.78 | convolution fusion | flops 1610858496 | bytes 8388608 | tf_op jit(solution)/shard_map/...km,mj->...kj/dot_general | solution.py:47
  135.0 6.9 %subtract_bitcast_fusion = f32[128,4,128,16]{0,2,3,1:T(8,128)S(1)} fusion(f32[128,4,16,128]{0,3,2,1:T(8,128)S(1)} %fusion.52, f32[128,4,16,128]{3,2,1,0:T(8,128)S(1)} %get-tuple-element.9), kind=kOutput, calls=%fused_computation.59 | convolution fusion | flops 1611890688 | bytes 12582912 | tf_op jit(solution)/shard_map/...km,mj->...kj/dot_general | solution.py:47
  146.4 9.2 %fusion.50 = f32[128,4,16,128]{0,3,2,1:T(8,128)S(1)} fusion(f32[128,4,16,128]{3,2,1,0:T(8,128)} %copy-done.5), kind=kOutput, calls=%fused_computation.76 | convolution fusion | flops 1610842112 | bytes 8388608 | tf_op jit(solution)/shard_map/...km,mj->...kj/dot_general | solution.py:47
  155.6 6.5 %add_bitcast_fusion = f32[128,4,128,16]{0,2,3,1:T(8,128)S(1)} fusion(f32[128,4,16,128]{0,3,2,1:T(8,128)S(1)} %fusion.50, f32[128,4,16,128]{3,2,1,0:T(8,128)S(1)} %copy-done.4), kind=kOutput, calls=%fused_computation.58 | convolution fusion | flops 1611907072 | bytes 12582912 | tf_op jit(solution)/shard_map/...km,mj->...kj/dot_general | solution.py:47
  166.6 10.4 %reduce-scatter.5.cloned.1.call-done = f32[128,4,1024]{0,2,1:T(8,128)} async-done(((f32[128,4,2048]{0,2,1:T(8,128)}), f32[128,4,1024]{0,2,1:T(8,128)}) %reduce-scatter.5.cloned.1.call-update) | async-done | bytes 2097168 | tf_op jit(solution)/shard_map/reduce_scatter | solution.py:109
  179.6 5.1 copy.125
  184.7 7.0 %all-to-all-start.2 = ((f32[2,128,4,1024]{1,2,0,3:T(4,128)}), f32[2,128,4,1024]{1,2,0,3:T(4,128)}, u32[]{:S(2)}, u32[]{:S(2)}) async-start(f32[2,128,4,1024]{1,2,0,3:T(4,128)} %copy.125), calls=%async_computation.4 | async-start | bytes 8388608 | tf_op jit(solution)/shard_map/all_to_all | solution.py:111
  193.3 78.7 %all-to-all-done.2 = f32[2,128,4,1024]{1,2,0,3:T(4,128)} async-done(((f32[2,128,4,1024]{1,2,0,3:T(4,128)}), f32[2,128,4,1024]{1,2,0,3:T(4,128)}, u32[]{:S(2)}, u32[]{:S(2)}) %all-to-all-start.2) | async-done | bytes 4194336 | tf_op jit(solution)/shard_map/all_to_all | solution.py:111
  298.4 5.6 add_bitcast_fusion.1
  308.5 8.8 %fusion.34 = (f32[4,64,16,128]{1,3,2,0:T(8,128)}, f32[4,64,16,128]{1,3,2,0:T(8,128)}) fusion(f32[64,16,128]{0,2,1:T(8,128)S(1)} %copy-done.15, f32[64,16,128]{0,2,1:T(8,128)S(1)} %get-tuple-element.17, f32[4,64,16,128]{1,3,2,0:T(8,128)} %bitcast.327, f32[4,64,16,128]{1,3,2,0:T(8,128)} %bitcast.325), kind=kLoop, calls=%fused_computation.48 | loop fusion | flops 3145728 | bytes 9437184 | tf_op jit(solution)/shard_map/sub | solution.py:126
  349.9 5.6 multiply_bitcast_fusion.2
  364.1 15.3 %copy.182 = f32[2,2048,4,64]{3,2,0,1:T(4,128)} copy(f32[2,2048,4,64]{3,1,2,0:T(8,128)S(1)} %maximum_bitcast_fusion) | data formatting | bytes 8388608 | tf_op jit(solution)/shard_map/transpose | solution.py:129
  379.4 14.6 %reshape.425 = f32[16,1,65536]{2,1,0:T(1,128)} reshape(f32[2048,2,4,64]{3,2,1,0:T(4,128)} %bitcast.315) | data formatting | bytes 8388608
  393.9 113.7 %all_to_all.71 = f32[16,1,65536]{2,1,0:T(1,128)} all-to-all(f32[16,1,65536]{2,1,0:T(1,128)} %reshape.425), channel_id=1, replica_groups=mesh['trans'=16,'los'=2] {'trans'}, dimensions={0} | all-to-all | bytes 8388608 | tf_op jit(solution)/shard_map/all_to_all | solution.py:140
  508.3 13.8 %reduce.2 = f32[16,65536]{1,0:T(8,128)} reduce(f32[16,1,65536]{2,1,0:T(1,128)} %all_to_all.71, f32[]{:T(128)} %broadcast.790), dimensions={1}, to_apply=%all_to_all.61.reduce_sub_computation | reduce | bytes 8388612 | tf_op jit(solution)/shard_map/all_to_all | solution.py:140
  522.1 9.3 %reshape.426 = f32[2048,2,4,64]{3,2,1,0:T(4,128)} reshape(f32[16,65536]{1,0:T(8,128)} %reduce.2) | data formatting | bytes 8388608
  531.4 8.5 %copy.160 = f32[2,16,128,4,64]{2,4,1,3,0:T(8,128)} copy(f32[2,16,128,4,64]{4,3,0,2,1:T(4,128)} %bitcast.314) | data formatting | bytes 8388608 | tf_op jit(solution)/shard_map/all_to_all | solution.py:140
  539.8 4.8 slice_bitcast_fusion.1
  548.6 6.8 %copy.139 = f32[2,2,64,4,1024]{4,2,3,1,0:T(8,128)} copy(f32[2,2,64,4,1024]{2,4,3,1,0:T(8,128)} %pad_maximum_fusion) | data formatting | bytes 8388608 | tf_op jit(solution)/shard_map/stack | solution.py:132
  555.3 8.7 %all_to_all.72 = f32[2,2,64,4,1024]{4,2,3,1,0:T(8,128)S(1)} all-to-all(f32[2,2,64,4,1024]{4,2,3,1,0:T(8,128)} %copy.139), channel_id=1, replica_groups=mesh['trans'=16,'los'=2] {'los'}, dimensions={0} | all-to-all | bytes 8388608 | tf_op jit(solution)/shard_map/all_to_all | solution.py:131
  599.5 4.8 copy.142
  604.2 5.6 multiply_bitcast_fusion
  609.8 4.8 copy.143
  614.6 7.2 %maximum_bitcast_fusion.1 = f32[2,4,64,2048]{2,3,1,0:T(8,128)} fusion(f32[1,64,4,2048]{1,3,2,0:T(8,128)} %bitcast.330, f32[1,64,4,2048]{1,3,2,0:T(8,128)} %bitcast.326), kind=kLoop, calls=%fused_computation.12 | loop fusion | flops 1048576 | bytes 8388608 | tf_op jit(solution)/shard_map/transpose | solution.py:143
  621.8 6.8 %copy.144 = f32[2,4,64,2048]{3,2,1,0:T(8,128)} copy(f32[2,4,64,2048]{2,3,1,0:T(8,128)} %maximum_bitcast_fusion.1) | data formatting | bytes 8388608 | tf_op jit(solution)/shard_map/transpose | solution.py:143
  (126 shorter events, 167.6 us)
Async XLA Ops:
  8.9 21.6 %copy-start.19 = (s32[2]{0:T(128)S(1)}, s32[2]{0:T(128)}, u32[]{:S(2)}) copy-start(s32[2]{0:T(128)} %param.9) | copy-start | bytes 28
  8.9 22.8 %copy-start.16 = (f32[2,2048]{1,0:T(2,128)S(1)}, f32[2,2048]{1,0:T(2,128)}, u32[]{:S(2)}) copy-start(f32[2,2048]{1,0:T(2,128)} %param.8) | copy-start | bytes 49156
  8.9 22.8 %copy-start.17 = (f32[2,2048]{1,0:T(2,128)S(1)}, f32[2,2048]{1,0:T(2,128)}, u32[]{:S(2)}) copy-start(f32[2,2048]{1,0:T(2,128)} %param.7) | copy-start | bytes 49156
  21.9 23.6 %all-to-all-start = ((bf16[16,2,8192]{2,1,0:T(2,128)(2,1)}), bf16[16,2,8192]{2,1,0:T(2,128)(2,1)S(1)}, u32[]{:S(2)}, u32[]{:S(2)}) async-start(bf16[16,2,8192]{2,1,0:T(2,128)(2,1)} %reshape.421), calls=%async_computation | async-start | bytes 1048576 | tf_op jit(solution)/shard_map/all_to_all | solution.py:73
  69.7 16.9 %copy-start.20 = (s32[2]{0:T(128)S(1)}, s32[2]{0:T(128)}, u32[]{:S(2)}) copy-start(s32[2]{0:T(128)} %param.10) | copy-start | bytes 28
  69.7 18.2 %copy-start.18 = (f32[4,2]{0,1:T(2,128)S(1)}, f32[4,2]{0,1:T(2,128)}, u32[]{:S(2)}) copy-start(f32[4,2]{0,1:T(2,128)} %param.11) | copy-start | bytes 100
  82.6 18.4 %all-to-all-start.1 = ((bf16[16,2,8192]{2,1,0:T(2,128)(2,1)}), bf16[16,2,8192]{2,1,0:T(2,128)(2,1)S(1)}, u32[]{:S(2)}, u32[]{:S(2)}) async-start(bf16[16,2,8192]{2,1,0:T(2,128)(2,1)} %reshape.423), calls=%async_computation.1 | async-start | bytes 1048576 | tf_op jit(solution)/shard_map/all_to_all | solution.py:97
  86.5 80.1 %reduce-scatter.3.cloned.1.call-start = ((), (), s32[]{:S(2)}) async-start(), calls=%async_computation.7 | async-start | bytes 6291456 | tf_op jit(solution)/shard_map/reduce_scatter | solution.py:108
  128.5 6.5 %copy-start.5 = (f32[128,4,16,128]{3,2,1,0:T(8,128)}, f32[128,4,16,128]{3,2,1,0:T(8,128)S(1)}, u32[]{:S(2)}) copy-start(f32[128,4,16,128]{3,2,1,0:T(8,128)S(1)} %get-tuple-element.10) | copy-start | bytes 12582916
  128.5 6.5 %copy-start.3 = (f32[128,4,16,128]{3,2,1,0:T(8,128)}, f32[128,4,16,128]{3,2,1,0:T(8,128)S(1)}, u32[]{:S(2)}) copy-start(f32[128,4,16,128]{3,2,1,0:T(8,128)S(1)} %get-tuple-element.9) | copy-start | bytes 12582916
  146.3 30.7 %reduce-scatter.5.cloned.1.call-start = ((), (), s32[]{:S(2)}) async-start(), calls=%async_computation.8 | async-start | bytes 6291456 | tf_op jit(solution)/shard_map/reduce_scatter | solution.py:109
  146.4 9.2 %copy-start.4 = (f32[128,4,16,128]{3,2,1,0:T(8,128)S(1)}, f32[128,4,16,128]{3,2,1,0:T(8,128)}, u32[]{:S(2)}) copy-start(f32[128,4,16,128]{3,2,1,0:T(8,128)} %copy-done.3) | copy-start | bytes 12582916
  184.7 87.3 %all-to-all-start.2 = ((f32[2,128,4,1024]{1,2,0,3:T(4,128)}), f32[2,128,4,1024]{1,2,0,3:T(4,128)}, u32[]{:S(2)}, u32[]{:S(2)}) async-start(f32[2,128,4,1024]{1,2,0,3:T(4,128)} %copy.125), calls=%async_computation.4 | async-start | bytes 8388608 | tf_op jit(solution)/shard_map/all_to_all | solution.py:111
  284.7 5.8 copy-start.1
  304.0 4.5 copy-start.15
  320.4 3.3 copy-start.6
  326.9 1.3 copy-start.8
  328.3 2.0 copy-start.13
  330.2 3.7 copy-start.7
  335.9 5.6 copy-start.2
  571.7 3.3 copy-start.9
  571.7 3.3 copy-start.14
  581.1 1.3 copy-start.11
  582.4 2.0 copy-start.12
  584.4 3.7 copy-start.10
  590.1 5.6 copy-start
Sparse Core Ops, SparseCore 0:
  146.4 10.2 reduce-scatter.2
  166.7 10.2 reduce-scatter.4
